TPU v7x, 128 devices: a whole 4x4x4 slice. The times are simulated.
128 devices in a mesh: row: 4 (over x_hi, core), col: 32 (over z, y, x_lo).
Axes of the slice: x: 4 (x_hi: 2, x_lo: 2; x = x_hi * 2 + x_lo), y: 4, z: 4, core: 2. Of those that a mesh axis runs over, the one named last changes fastest.
Arguments:
- rows: bfloat16 [4096, 4096], P(('row', 'col')), may hold values from -6 to 6
- task_ids: int32 [4096], P(('row', 'col')), may hold values from 0 to 8, as said below
- task_embed: bfloat16 [8, 4096], replicated, may hold values from -6 to 6
- norm_gain: float32 [4, 4096], replicated, may hold values from 0.1 to 1.9
- layer_weight: bfloat16 [4, 4096, 4096], P(None, None, 'col'), may hold values from -0.09375 to 0.09375
Outputs:
- packed_out: bfloat16 [4096, 4096], P('row', 'col')
Inputs may be any that keep to these rules, and one draw needn't show every extreme that they name: `task_ids`: 8 marks an empty row, smaller values name a task.
All inputs are finite; a program needn't handle non-finite values.
Results may differ from a plain program's by a relative error of at most 0.008.
Values may be sent and summed in bfloat16 or wider, within the bound.
A program may use at most 128 MiB of HBM per device.

v0:
```python
import jax
import jax.numpy as jnp
from jax import lax
from jax.sharding import Mesh
from jax.sharding import PartitionSpec as P

COL = ("col_0", "col_1", "col_2")
ROW_COL = ("row", "col_0", "col_1", "col_2")
epsilon = 1e-06


def from_everyone(x, axis):
    size = lax.axis_size(axis)
    return lax.all_to_all(jnp.broadcast_to(x[None], (size, *x.shape)), axis, 0, 0, tiled=True)


def folded_in_pairs(pieces, combine):
    while len(jax.tree.leaves(pieces)[0]) > 1:
        pieces = jax.vmap(combine)(*(pieces[side::2] for side in (0, 1)))
    return pieces[0]


def entering(x, axis, combine, identity):
    size, index = (lax.axis_size(axis), lax.axis_index(axis))
    passed = jnp.arange(size) < index

    def kept(part, zero, own):
        part = jnp.where(
            passed.reshape(-1, *(1 for _ in own.shape)), part, jnp.asarray(zero, own.dtype)
        )
        return part

    pieces = from_everyone(x, axis)
    return folded_in_pairs(kept(pieces, identity, x), combine)


def taken_together(x, axis):
    return from_everyone(x, axis).sum(axis=0)


def rows_for(lines, size):
    spare = -len(lines) % size
    return jnp.pad(lines, [(0, spare)] + [(0, 0)] * (lines.ndim - 1))


def own_block(blocks, axes, turns):
    dims = [lax.axis_size(a) for a in axes]
    blocks = blocks.reshape(*dims, *blocks.shape[1:])
    blocks = blocks.transpose(*turns, *range(len(axes), blocks.ndim))
    blocks = blocks.reshape(-1, *blocks.shape[len(axes) :])
    for k in turns:
        blocks = lax.psum_scatter(blocks, axes[k], scatter_dimension=0, tiled=True)
    return blocks[0]


def all_blocks(x, axes, turns):
    blocks = x
    for k in turns:
        blocks = lax.all_gather(blocks, axes[k])
    done = turns[::-1]
    back = [done.index(k) for k in range(len(axes))]
    blocks = blocks.transpose(*back, *range(len(axes), blocks.ndim))
    return blocks.reshape(-1, *x.shape)


def total_of(x, axes, turns):
    size, lines = (lax.axis_size(axes), x.reshape(-1, *x.shape[1:][-1:]))
    blocks = rows_for(lines, size).reshape(size, -1, *lines.shape[1:])
    own = own_block(blocks, axes, turns)
    whole = all_blocks(own, axes, turns[::-1]).reshape(-1, *lines.shape[1:])
    return whole[: len(lines)].reshape(x.shape)


def add_counts(earlier, later):
    return earlier + later


def activate_rows(hidden, gain):
    total_rows = hidden.shape[0]
    width = hidden.shape[1]
    block_rows = min(512, total_rows)

    def one_block(block):
        values = block.astype(jnp.float32)
        inverse_rms = lax.rsqrt(jnp.mean(values * values, axis=1, keepdims=True) + epsilon)
        return jax.nn.silu(values * inverse_rms * gain[None, :]).astype(jnp.bfloat16)

    blocks = hidden.reshape(total_rows // block_rows, block_rows, width)
    return lax.map(one_block, blocks).reshape(total_rows, width)


def shards(rows, task_ids, task_embed, norm_gain, layer_weight):
    row_count = rows.shape[0]
    width = rows.shape[1]
    task_count = task_embed.shape[0]
    row_devices = lax.axis_size("row")
    col_devices = lax.axis_size(COL)
    capacity = row_count // row_devices + task_count
    slots_group = row_count * col_devices
    task_range = jnp.arange(task_count, dtype=jnp.int32)
    member = (task_ids[:, None] == task_range[None, :]).astype(jnp.int32)
    counts = jnp.sum(member, axis=0)
    zero_counts = jnp.zeros_like(counts)
    before_col = entering(counts, COL, add_counts, zero_counts)
    row_total = taken_together(counts, COL)
    before_row = entering(row_total, "row", add_counts, zero_counts)
    totals = taken_together(row_total, "row")
    before = before_row + before_col
    task_base = jnp.cumsum(totals) - totals
    positions = jnp.arange(row_count, dtype=jnp.int32)
    earlier_mask = positions[None, :] < positions[:, None]
    same_task = task_ids[:, None] == task_ids[None, :]
    task_rank = jnp.sum((same_task & earlier_mask).astype(jnp.int32), axis=1)
    row_live = task_ids < task_count
    packed_pos = (
        jnp.sum(member * (task_base + before)[None, :], axis=1).astype(jnp.int32) + task_rank
    )
    target_row = packed_pos % row_devices
    slot_index = packed_pos // row_devices
    before_pos = packed_pos[None, :] < packed_pos[:, None]
    same_target = (target_row[:, None] == target_row[None, :]) & row_live[None, :]
    within = jnp.sum((same_target & before_pos).astype(jnp.int32), axis=1)
    send_at = jnp.where(row_live, target_row * capacity + within, -1)
    buffer_range = jnp.arange(row_devices * capacity, dtype=jnp.int32)
    select = buffer_range[:, None] == send_at[None, :]
    send_rows = jnp.dot(
        select.astype(jnp.bfloat16), rows, preferred_element_type=jnp.float32
    ).astype(jnp.bfloat16)
    send_rows = send_rows.reshape(row_devices, capacity, width)
    send_slots = jnp.sum(jnp.where(select, slot_index[None, :] + 1, 0), axis=1) - 1
    send_slots = send_slots.reshape(row_devices, capacity)
    got_rows, got_slots = (
        lax.all_to_all(send_rows, "row", split_axis=0, concat_axis=0, tiled=True),
        lax.all_to_all(send_slots, "row", split_axis=0, concat_axis=0, tiled=True),
    )
    got_rows = got_rows.reshape(row_devices * capacity, width)
    got_slots = got_slots.reshape(row_devices * capacity)
    slot_range = jnp.arange(slots_group, dtype=jnp.int32)
    placing = (slot_range[:, None] == got_slots[None, :]).astype(jnp.bfloat16)
    local_part = jnp.dot(placing, got_rows, preferred_element_type=jnp.float32).astype(jnp.bfloat16)
    placed = total_of(local_part, COL, (0, 1, 2)).astype(jnp.float32)
    group_index = lax.axis_index("row")
    slot_pos = slot_range * row_devices + group_index
    in_task = (slot_pos[:, None] >= task_base[None, :]) & (
        slot_pos[:, None] < (task_base + totals)[None, :]
    )
    task_term = jnp.dot(
        in_task.astype(jnp.bfloat16), task_embed, preferred_element_type=jnp.float32
    )
    hidden = (placed + task_term).astype(jnp.bfloat16)
    part_width = width // col_devices
    column = lax.axis_index(COL) * part_width
    layers = layer_weight.shape[0]
    result = hidden
    for layer_index in range(layers):
        active = activate_rows(hidden, norm_gain[layer_index])
        update = jnp.dot(active, layer_weight[layer_index], preferred_element_type=jnp.float32)
        own_cols = lax.dynamic_slice_in_dim(hidden, column, part_width, 1).astype(jnp.float32)
        result = (own_cols + update).astype(jnp.bfloat16)
        if layer_index + 1 < layers:
            hidden = lax.all_gather(result, COL, axis=1, tiled=True)
    return result


def solution(mesh):
    finer = Mesh(
        mesh.devices.reshape(mesh.shape["row"], 4, 4, 2), ("row", "col_0", "col_1", "col_2")
    )
    return jax.shard_map(
        shards,
        mesh=finer,
        in_specs=(P(ROW_COL, None), P(ROW_COL), P(), P(), P(None, None, COL)),
        out_specs=P("row", COL),
        check_vma=False,
    )
```

profile of v0, /device:TPU:0, one launch (start us, length us, event | category | flops | bytes accessed | tf_op | source)
XLA Modules:
  0.0 1077.1 jit_solution(16607815354569057039)
XLA Ops:
  7.9 9.4 all-to-all-start
  18.9 6.6 all-to-all-done
  51.6 9.0 all-to-all-done.3
  66.2 76.0 %reduce-scatter.4.cloned.1.call-done = bf16[8,32,4096]{2,1,0:T(8,128)(2,1)} async-done(((bf16[32,32,4096]{2,1,0:T(8,128)(2,1)}), bf16[8,32,4096]{2,1,0:T(8,128)(2,1)}) %reduce-scatter.4.cloned.1.call-update) | async-done | bytes 2097168 | tf_op jit(solution)/shard_map/reduce_scatter | solution.py:52
  142.3 31.7 %reduce-scatter.6.cloned.1.call-done = bf16[2,32,4096]{2,1,0:T(8,128)(2,1)} async-done(((bf16[8,32,4096]{2,1,0:T(8,128)(2,1)}), bf16[2,32,4096]{2,1,0:T(8,128)(2,1)}) %reduce-scatter.6.cloned.1.call-update) | async-done | bytes 524304 | tf_op jit(solution)/shard_map/reduce_scatter | solution.py:52
  174.1 19.2 %reduce-scatter.8.cloned.1.call-done = bf16[1,32,4096]{2,1,0:T(8,128)(2,1)} async-done(((bf16[2,32,4096]{2,1,0:T(8,128)(2,1)}), bf16[1,32,4096]{2,1,0:T(8,128)(2,1)}) %reduce-scatter.8.cloned.1.call-update) | async-done | bytes 262160 | tf_op jit(solution)/shard_map/reduce_scatter | solution.py:52
  193.2 10.2 all_gather.24
  203.6 32.5 %all-gather.14.cloned.1.call-done = bf16[8,32,4096]{2,1,0:T(8,128)(2,1)} async-done(((bf16[2,32,4096]{2,1,0:T(8,128)(2,1)}), bf16[8,32,4096]{2,1,0:T(8,128)(2,1)}) %all-gather.14.cloned.1.call-update) | async-done | bytes 2097168 | tf_op jit(solution)/shard_map/all_gather | solution.py:59
  236.4 84.5 %all-gather.16.cloned.1.call-done = bf16[16,2,32,4096]{3,2,1,0:T(8,128)(2,1)} async-done(((bf16[4,2,32,4096]{3,2,1,0:T(8,128)(2,1)}), bf16[16,2,32,4096]{3,2,1,0:T(8,128)(2,1)}) %all-gather.16.cloned.1.call-update) | async-done | bytes 8388624 | tf_op jit(solution)/shard_map/all_gather | solution.py:59
  320.9 9.1 fusion.36
  334.2 17.3 %while.40 = (s32[]{:T(128)}, bf16[2,512,4096]{2,1,0:T(8,128)(2,1)}, bf16[2,512,4096]{2,1,0:T(8,128)(2,1)}, f32[1,4096]{1,0:T(1,128)S(1)}, s32[]{:T(128)}) while((s32[]{:T(128)}, bf16[2,512,4096]{2,1,0:T(8,128)(2,1)}, bf16[2,512,4096]{2,1,0:T(8,128)(2,1)}, f32[1,4096]{1,0:T(1,128)S(1)}, s32[]{:T(128)}) %tuple.89), condition=%wide.region_13.14_spmd, body=%wide.region_11.13_spmd.sunk | while | flops 23069184 | bytes 12608065 | solution.py:89
  345.9 5.6 fusion.78
  351.5 6.8 fusion.37
  358.6 209.7 %all-gather.8.cloned.1.call-done = bf16[1024,4096]{1,0:T(8,128)(2,1)} async-done(((bf16[1024,128]{1,0:T(8,128)(2,1)}), bf16[1024,4096]{1,0:T(8,128)(2,1)}) %all-gather.8.cloned.1.call-update) | async-done | bytes 8388624 | tf_op jit(solution)/shard_map/all_gather | solution.py:161
  572.6 17.3 %while.41 = (s32[]{:T(128)}, bf16[2,512,4096]{2,1,0:T(8,128)(2,1)}, bf16[2,512,4096]{2,1,0:T(8,128)(2,1)}, f32[1,4096]{1,0:T(1,128)S(1)}, s32[]{:T(128)}) while((s32[]{:T(128)}, bf16[2,512,4096]{2,1,0:T(8,128)(2,1)}, bf16[2,512,4096]{2,1,0:T(8,128)(2,1)}, f32[1,4096]{1,0:T(1,128)S(1)}, s32[]{:T(128)}) %tuple.91), condition=%wide.region_16.17_spmd, body=%wide.region_14.16_spmd.sunk | while | flops 23069184 | bytes 12608065 | solution.py:89
  584.3 5.6 fusion.80
  589.9 6.8 fusion.38
  597.0 208.1 %all-gather.10.cloned.1.call-done = bf16[1024,4096]{1,0:T(8,128)(2,1)} async-done(((bf16[1024,128]{1,0:T(8,128)(2,1)}), bf16[1024,4096]{1,0:T(8,128)(2,1)}) %all-gather.10.cloned.1.call-update) | async-done | bytes 8388624 | tf_op jit(solution)/shard_map/all_gather | solution.py:161
  809.4 17.3 %while.42 = (s32[]{:T(128)}, bf16[2,512,4096]{2,1,0:T(8,128)(2,1)}, bf16[2,512,4096]{2,1,0:T(8,128)(2,1)}, f32[1,4096]{1,0:T(1,128)S(1)}, s32[]{:T(128)}) while((s32[]{:T(128)}, bf16[2,512,4096]{2,1,0:T(8,128)(2,1)}, bf16[2,512,4096]{2,1,0:T(8,128)(2,1)}, f32[1,4096]{1,0:T(1,128)S(1)}, s32[]{:T(128)}) %tuple.92), condition=%wide.region_19.20_spmd, body=%wide.region_17.19_spmd.sunk | while | flops 23069184 | bytes 12608065 | solution.py:89
  821.1 5.6 fusion.82
  826.7 6.8 fusion.39
  833.5 208.4 %all-gather.12.cloned.1.call-done = bf16[1024,4096]{1,0:T(8,128)(2,1)} async-done(((bf16[1024,128]{1,0:T(8,128)(2,1)}), bf16[1024,4096]{1,0:T(8,128)(2,1)}) %all-gather.12.cloned.1.call-update) | async-done | bytes 8388624 | tf_op jit(solution)/shard_map/all_gather | solution.py:161
  1046.2 17.3 %while.43 = (s32[]{:T(128)}, bf16[2,512,4096]{2,1,0:T(8,128)(2,1)}, bf16[2,512,4096]{2,1,0:T(8,128)(2,1)}, f32[1,4096]{1,0:T(1,128)S(1)}, s32[]{:T(128)}) while((s32[]{:T(128)}, bf16[2,512,4096]{2,1,0:T(8,128)(2,1)}, bf16[2,512,4096]{2,1,0:T(8,128)(2,1)}, f32[1,4096]{1,0:T(1,128)S(1)}, s32[]{:T(128)}) %tuple.90), condition=%wide.region_22.23_spmd, body=%wide.region_20.22_spmd.sunk | while | flops 23069184 | bytes 12608065 | solution.py:89
  1063.5 6.8 fusion.40
  (98 shorter events, 105.3 us)
Async XLA Ops:
  6.5 35.1 %copy-start = (bf16[32,4096]{1,0:T(8,128)(2,1)S(1)}, bf16[32,4096]{1,0:T(8,128)(2,1)}, u32[]{:S(2)}) copy-start(bf16[32,4096]{1,0:T(8,128)(2,1)} %param.13) | copy-start | bytes 786436
  7.9 17.6 %all-to-all-start = ((s32[32,1,8]{2,1,0:T(1,128)}), s32[32,1,8]{2,1,0:T(1,128)S(1)}, u32[]{:S(2)}, u32[]{:S(2)}) async-start(s32[32,1,8]{2,1,0:T(1,128)} %broadcast_in_dim.43), calls=%async_computation | async-start | bytes 32768 | tf_op jit(solution)/shard_map/all_to_all | solution.py:14
  26.4 9.2 all-to-all-start.1
  38.4 8.4 all-to-all-start.2
  46.9 13.8 %all-to-all-start.3 = ((bf16[4,16,4096]{2,1,0:T(8,128)(2,1)}), bf16[4,16,4096]{2,1,0:T(8,128)(2,1)S(1)}, u32[]{:S(2)}, u32[]{:S(2)}) async-start(bf16[4,16,4096]{2,1,0:T(8,128)(2,1)} %bitcast.11), calls=%async_computation.3 | async-start | bytes 1048576 | tf_op jit(solution)/shard_map/all_to_all | solution.py:133
  50.3 91.9 %reduce-scatter.4.cloned.1.call-start = ((), (), s32[]{:S(2)}) async-start(), calls=%async_computation.7 | async-start | bytes 10485760 | tf_op jit(solution)/shard_map/reduce_scatter | solution.py:52
  66.2 170.2 %copy-start.3 = (f32[4,4096]{1,0:T(4,128)S(1)}, f32[4,4096]{1,0:T(4,128)}, u32[]{:S(2)}) copy-start(f32[4,4096]{1,0:T(4,128)} %param.16) | copy-start | bytes 196612
  66.2 254.7 %copy-start.2 = (bf16[8,4096]{1,0:T(8,128)(2,1)S(1)}, bf16[8,4096]{1,0:T(8,128)(2,1)}, u32[]{:S(2)}) copy-start(bf16[8,4096]{1,0:T(8,128)(2,1)} %param.15) | copy-start | bytes 196612
  66.2 107.8 %reduce-scatter.6.cloned.1.call-start = ((), (), s32[]{:S(2)}) async-start(), calls=%async_computation.8 | async-start | bytes 2621440 | tf_op jit(solution)/shard_map/reduce_scatter | solution.py:52
  142.3 51.0 %reduce-scatter.8.cloned.1.call-start = ((), (), s32[]{:S(2)}) async-start(), calls=%async_computation.9 | async-start | bytes 786432 | tf_op jit(solution)/shard_map/reduce_scatter | solution.py:52
  174.0 62.0 %all-gather.14.cloned.1.call-start = ((), (), s32[]{:S(2)}) async-start(), calls=%async_computation.13 | async-start | bytes 2621440 | tf_op jit(solution)/shard_map/all_gather | solution.py:59
  203.5 117.4 %all-gather.16.cloned.1.call-start = ((), (), s32[]{:S(2)}) async-start(), calls=%async_computation.14 | async-start | bytes 10485760 | tf_op jit(solution)/shard_map/all_gather | solution.py:59
  236.1 332.3 %all-gather.8.cloned.1.call-start = ((), (), s32[]{:S(2)}) async-start(), calls=%async_computation.10 | async-start | bytes 8650752 | tf_op jit(solution)/shard_map/all_gather | solution.py:161
  358.3 446.8 %all-gather.10.cloned.1.call-start = ((), (), s32[]{:S(2)}) async-start(), calls=%async_computation.11 | async-start | bytes 8650752 | tf_op jit(solution)/shard_map/all_gather | solution.py:161
  596.7 445.2 %all-gather.12.cloned.1.call-start = ((), (), s32[]{:S(2)}) async-start(), calls=%async_computation.12 | async-start | bytes 8650752 | tf_op jit(solution)/shard_map/all_gather | solution.py:161
  1063.5 6.8 copy-start.1
Sparse Core Ops, SparseCore 0:
  66.3 75.9 reduce-scatter.3
  144.7 29.2 reduce-scatter.5
  176.4 16.8 reduce-scatter.7
  203.6 32.3 all-gather.13
  237.6 83.2 all-gather.15
  358.4 209.8 all-gather.7
  596.8 208.2 all-gather.9
  833.6 208.2 all-gather.11
where the time goes:
time: 1080 us
  waiting for transfers between devices  895 us (83%)
  other arithmetic  74.6 us (7%)
  matrix products  42.9 us (4%)
  starting transfers between devices  21 us (2%)
  local copies, waits for them, and re-layouts  19.8 us (2%)
  between operations  13.6 us (1%)
    all_gather x3, waiting for transfers between devices, shards(): hidden = lax.all_gather(result, COL, axis=1, tiled=True)  626 us
    reduce_scatter x3, waiting for transfers between devices, own_block(): blocks = lax.psum_scatter(blocks, axes[k], scatter_dimension=0, tiled=True)  127 us
    all_gather x2, waiting for transfers between devices, all_blocks(): blocks = lax.all_gather(blocks, axes[k])  117 us
    dynamic_update_slice x8, other arithmetic, activate_rows(): return lax.map(one_block, blocks).reshape(total_rows, width)  44.6 us
    dot_general x4, matrix products, shards(): jnp.dot(active, layer_weight[layer_index], preferred_element_type=jnp.flo...  27.1 us
    reduce_sum x8, other arithmetic, one_block(): jnp.mean(values * values, axis=1, keepdims=True) + epsilon  24.6 us
  transfers between devices with their start and end apart: 12, of which 12 were waited for; matrix products, arithmetic and copies ran while one was open for 0% of the time, Pallas kernels for 0%

commit v1 on v0

--- a/solution.py
+++ b/solution.py
@@ -158,7 +158,10 @@
         own_cols = lax.dynamic_slice_in_dim(hidden, column, part_width, 1).astype(jnp.float32)
         result = (own_cols + update).astype(jnp.bfloat16)
         if layer_index + 1 < layers:
-            hidden = lax.all_gather(result, COL, axis=1, tiled=True)
+            hidden = jnp.concatenate(
+                lax.all_to_all(jnp.stack([result for _ in range(lax.axis_size(COL))]), COL, 0, 0),
+                axis=1,
+            )
     return result
 
 

time: 1080 us -> 939 us (0.87)
  waiting for transfers between devices: 895 us -> 503 us
  blocking collectives: 10.2 us -> 124 us
  local copies, waits for them, and re-layouts: 19.8 us -> 131 us
  starting transfers between devices: 21 us -> 44.6 us
    all_gather x3 -> x0, waiting for transfers between devices: 626 us -> none  [shards(): hidden = lax.all_gather(result, COL, axis=1, tiled=True)]
    all_to_all x0 -> x2, waiting for transfers between devices: none -> 235 us  [shards(): lax.all_to_all(jnp.stack([result for _ in range(lax.axis_size(COL))]), CO...]
    all_to_all x0 -> x1, blocking collectives: none -> 114 us  [shards(): lax.all_to_all(jnp.stack([result for _ in range(lax.axis_size(COL))]), CO...]
    reshape x0 -> x6, local copies, waits for them, and re-layouts: none -> 59.5 us  [shards(): jnp.concatenate(lax.all_to_all(jnp.stack([result for _ in range(lax.axis_...]
    another operation x4 -> x10, local copies, waits for them, and re-layouts: 17 us -> 69 us  [the longest x3 39.9 us: activate_rows(): blocks = hidden.reshape(total_rows // block_rows, block_rows, width)]
    all_to_all x0 -> x2, starting transfers between devices: none -> 24.2 us  [shards(): lax.all_to_all(jnp.stack([result for _ in range(lax.axis_size(COL))]), CO...]
  transfers between devices with their start and end apart: 12 -> 11, of which waited for: 12 -> 11; matrix products, arithmetic and copies ran while one was open for 0% -> 0% of each run, Pallas kernels for 0% -> 0%
where the time goes in v1:
time: 939 us; the launch traced here: 933 us
  waiting for transfers between devices  503 us (54%)
  local copies, waits for them, and re-layouts  131 us (14%)
  blocking collectives  124 us (13%)
  other arithmetic  74.6 us (8%)
  starting transfers between devices  44.6 us (5%)
  matrix products  40.8 us (4%)
  between operations  13.6 us (1%)
    all_to_all x2, waiting for transfers between devices, shards(): lax.all_to_all(jnp.stack([result for _ in range(lax.axis_size(COL))]), CO...  235 us
    reduce_scatter x3, waiting for transfers between devices, own_block(): blocks = lax.psum_scatter(blocks, axes[k], scatter_dimension=0, tiled=True)  127 us
    all_gather x2, waiting for transfers between devices, all_blocks(): blocks = lax.all_gather(blocks, axes[k])  117 us
    all_to_all x1, blocking collectives, shards(): lax.all_to_all(jnp.stack([result for _ in range(lax.axis_size(COL))]), CO...  114 us
    reshape x6, local copies, waits for them, and re-layouts, shards(): jnp.concatenate(lax.all_to_all(jnp.stack([result for _ in range(lax.axis_...  59.5 us
    dynamic_update_slice x8, other arithmetic, activate_rows(): return lax.map(one_block, blocks).reshape(total_rows, width)  44.6 us
    another operation x3, local copies, waits for them, and re-layouts, activate_rows(): blocks = hidden.reshape(total_rows // block_rows, block_rows, width)  39.9 us
    dot_general x4, matrix products, shards(): jnp.dot(active, layer_weight[layer_index], preferred_element_type=jnp.flo...  25 us
  transfers between devices with their start and end apart: 11, of which 11 were waited for; matrix products, arithmetic and copies ran while one was open for 0% of the time, Pallas kernels for 0%

profile of v1, /device:TPU:0, one launch (start us, length us, event | category | flops | bytes accessed | tf_op | source)
XLA Modules:
  0.0 933.2 jit_solution(4628540100985994374)
XLA Ops:
  7.9 9.4 %all-to-all-start = ((s32[32,1,8]{2,1,0:T(1,128)}), s32[32,1,8]{2,1,0:T(1,128)S(1)}, u32[]{:S(2)}, u32[]{:S(2)}) async-start(s32[32,1,8]{2,1,0:T(1,128)} %broadcast_in_dim.43), calls=%async_computation | async-start | bytes 32768 | tf_op jit(solution)/shard_map/all_to_all | solution.py:14
  51.6 9.0 all-to-all-done.3
  66.2 76.0 %reduce-scatter.4.cloned.1.call-done = bf16[8,32,4096]{2,1,0:T(8,128)(2,1)} async-done(((bf16[32,32,4096]{2,1,0:T(8,128)(2,1)}), bf16[8,32,4096]{2,1,0:T(8,128)(2,1)}) %reduce-scatter.4.cloned.1.call-update) | async-done | bytes 2097168 | tf_op jit(solution)/shard_map/reduce_scatter | solution.py:52
  142.3 31.7 %reduce-scatter.6.cloned.1.call-done = bf16[2,32,4096]{2,1,0:T(8,128)(2,1)} async-done(((bf16[8,32,4096]{2,1,0:T(8,128)(2,1)}), bf16[2,32,4096]{2,1,0:T(8,128)(2,1)}) %reduce-scatter.6.cloned.1.call-update) | async-done | bytes 524304 | tf_op jit(solution)/shard_map/reduce_scatter | solution.py:52
  174.1 19.2 %reduce-scatter.8.cloned.1.call-done = bf16[1,32,4096]{2,1,0:T(8,128)(2,1)} async-done(((bf16[2,32,4096]{2,1,0:T(8,128)(2,1)}), bf16[1,32,4096]{2,1,0:T(8,128)(2,1)}) %reduce-scatter.8.cloned.1.call-update) | async-done | bytes 262160 | tf_op jit(solution)/shard_map/reduce_scatter | solution.py:52
  193.2 10.2 %all_gather.15 = bf16[2,32,4096]{2,1,0:T(8,128)(2,1)} all-gather(bf16[1,32,4096]{2,1,0:T(8,128)(2,1)} %reduce-scatter.8.cloned.1.call-done), channel_id=1, replica_groups=mesh['row'=4,'col_0'=4,'col_1'=4,'col_2'=2] {'col_2'}, dimensions={0}, use_global_device_ids=true | all-gather | bytes 786432 | tf_op jit(solution)/shard_map/all_gather | solution.py:59
  203.7 32.3 %all-gather.5.cloned.1.call-done = bf16[8,32,4096]{2,1,0:T(8,128)(2,1)} async-done(((bf16[2,32,4096]{2,1,0:T(8,128)(2,1)}), bf16[8,32,4096]{2,1,0:T(8,128)(2,1)}) %all-gather.5.cloned.1.call-update) | async-done | bytes 2097168 | tf_op jit(solution)/shard_map/all_gather | solution.py:59
  236.2 84.7 %all-gather.7.cloned.1.call-done = bf16[16,2,32,4096]{3,2,1,0:T(8,128)(2,1)} async-done(((bf16[4,2,32,4096]{3,2,1,0:T(8,128)(2,1)}), bf16[16,2,32,4096]{3,2,1,0:T(8,128)(2,1)}) %all-gather.7.cloned.1.call-update) | async-done | bytes 8388624 | tf_op jit(solution)/shard_map/all_gather | solution.py:59
  320.9 9.1 fusion.36
  334.2 17.3 %while.40 = (s32[]{:T(128)}, bf16[2,512,4096]{2,1,0:T(8,128)(2,1)}, bf16[2,512,4096]{2,1,0:T(8,128)(2,1)}, f32[1,4096]{1,0:T(1,128)S(1)}, s32[]{:T(128)}) while((s32[]{:T(128)}, bf16[2,512,4096]{2,1,0:T(8,128)(2,1)}, bf16[2,512,4096]{2,1,0:T(8,128)(2,1)}, f32[1,4096]{1,0:T(1,128)S(1)}, s32[]{:T(128)}) %tuple.83), condition=%wide.region_13.14_spmd, body=%wide.region_11.13_spmd.sunk | while | flops 23069184 | bytes 12608065 | solution.py:89
  362.7 8.1 all-to-all-start.4
  370.8 122.6 %all-to-all-done.4 = bf16[32,1024,128]{2,1,0:T(8,128)(2,1)} async-done(((bf16[32,1024,128]{2,1,0:T(8,128)(2,1)}), bf16[32,1024,128]{2,1,0:T(8,128)(2,1)}, u32[]{:S(2)}, u32[]{:S(2)}) %all-to-all-start.4) | async-done | bytes 8388640 | tf_op jit(solution)/shard_map/all_to_all | solution.py:162
  493.4 12.0 %copy.25 = bf16[1024,32,128]{2,1,0:T(8,128)(2,1)} copy(bf16[1024,32,128]{2,0,1:T(8,128)(2,1)} %bitcast.20) | data formatting | bytes 16777216 | tf_op jit(solution)/shard_map/reshape | solution.py:161
  505.4 13.3 %reshape_reshape.10 = bf16[2,512,4096]{2,1,0:T(8,128)(2,1)} reshape(bf16[1024,32,128]{2,1,0:T(8,128)(2,1)} %copy.25) | data formatting | bytes 16777216 | tf_op jit(solution)/shard_map/reshape;reshape | solution.py:88
  523.0 17.8 %while.41 = (s32[]{:T(128)}, bf16[2,512,4096]{2,1,0:T(8,128)(2,1)}, bf16[2,512,4096]{2,1,0:T(8,128)(2,1)}, f32[1,4096]{1,0:T(1,128)S(1)}, s32[]{:T(128)}) while((s32[]{:T(128)}, bf16[2,512,4096]{2,1,0:T(8,128)(2,1)}, bf16[2,512,4096]{2,1,0:T(8,128)(2,1)}, f32[1,4096]{1,0:T(1,128)S(1)}, s32[]{:T(128)}) %tuple.64), condition=%wide.region_16.17_spmd, body=%wide.region_14.16_spmd.sunk | while | flops 23069184 | bytes 12608065 | solution.py:89
  559.7 16.1 %all-to-all-start.5 = ((bf16[32,1024,128]{2,1,0:T(8,128)(2,1)}), bf16[32,1024,128]{2,1,0:T(8,128)(2,1)}, u32[]{:S(2)}, u32[]{:S(2)}) async-start(bf16[32,1024,128]{2,1,0:T(8,128)(2,1)} %stack.7), calls=%async_computation.8 | async-start | bytes 16777216 | tf_op jit(solution)/shard_map/all_to_all | solution.py:162
  575.9 112.0 %all-to-all-done.5 = bf16[32,1024,128]{2,1,0:T(8,128)(2,1)} async-done(((bf16[32,1024,128]{2,1,0:T(8,128)(2,1)}), bf16[32,1024,128]{2,1,0:T(8,128)(2,1)}, u32[]{:S(2)}, u32[]{:S(2)}) %all-to-all-start.5) | async-done | bytes 8388640 | tf_op jit(solution)/shard_map/all_to_all | solution.py:162
  687.9 12.0 %copy.27 = bf16[1024,32,128]{2,1,0:T(8,128)(2,1)} copy(bf16[1024,32,128]{2,0,1:T(8,128)(2,1)} %bitcast.23) | data formatting | bytes 16777216 | tf_op jit(solution)/shard_map/reshape | solution.py:161
  699.9 13.3 %reshape_reshape.11 = bf16[2,512,4096]{2,1,0:T(8,128)(2,1)} reshape(bf16[1024,32,128]{2,1,0:T(8,128)(2,1)} %copy.27) | data formatting | bytes 16777216 | tf_op jit(solution)/shard_map/reshape;reshape | solution.py:88
  717.5 17.5 %while.42 = (s32[]{:T(128)}, bf16[2,512,4096]{2,1,0:T(8,128)(2,1)}, bf16[2,512,4096]{2,1,0:T(8,128)(2,1)}, f32[1,4096]{1,0:T(1,128)S(1)}, s32[]{:T(128)}) while((s32[]{:T(128)}, bf16[2,512,4096]{2,1,0:T(8,128)(2,1)}, bf16[2,512,4096]{2,1,0:T(8,128)(2,1)}, f32[1,4096]{1,0:T(1,128)S(1)}, s32[]{:T(128)}) %tuple.67), condition=%wide.region_19.20_spmd, body=%wide.region_17.19_spmd.sunk | while | flops 23069184 | bytes 12608065 | solution.py:89
  750.7 113.9 %all_to_all.46 = bf16[32,1024,128]{2,1,0:T(8,128)(2,1)} all-to-all(bf16[32,1024,128]{2,1,0:T(8,128)(2,1)S(1)} %stack.8), channel_id=1, replica_groups=mesh['row'=4,'col_0'=4,'col_1'=4,'col_2'=2] {'col_0','col_1','col_2'}, dimensions={0} | all-to-all | bytes 16777216 | tf_op jit(solution)/shard_map/all_to_all | solution.py:162
  864.7 12.0 %copy.29 = bf16[1024,32,128]{2,1,0:T(8,128)(2,1)} copy(bf16[1024,32,128]{2,0,1:T(8,128)(2,1)} %bitcast.78) | data formatting | bytes 16777216 | tf_op jit(solution)/shard_map/reshape | solution.py:161
  876.7 13.3 %reshape_reshape.12 = bf16[2,512,4096]{2,1,0:T(8,128)(2,1)} reshape(bf16[1024,32,128]{2,1,0:T(8,128)(2,1)} %copy.29) | data formatting | bytes 16777216 | tf_op jit(solution)/shard_map/reshape;reshape | solution.py:88
  894.2 17.5 %while.43 = (s32[]{:T(128)}, bf16[2,512,4096]{2,1,0:T(8,128)(2,1)}, bf16[2,512,4096]{2,1,0:T(8,128)(2,1)}, f32[1,4096]{1,0:T(1,128)S(1)}, s32[]{:T(128)}) while((s32[]{:T(128)}, bf16[2,512,4096]{2,1,0:T(8,128)(2,1)}, bf16[2,512,4096]{2,1,0:T(8,128)(2,1)}, f32[1,4096]{1,0:T(1,128)S(1)}, s32[]{:T(128)}) %tuple.70), condition=%wide.region_22.23_spmd, body=%wide.region_20.22_spmd.sunk | while | flops 23069184 | bytes 12608065 | solution.py:89
  (106 shorter events, 188.6 us)
Async XLA Ops:
  6.5 35.1 %copy-start = (bf16[32,4096]{1,0:T(8,128)(2,1)S(1)}, bf16[32,4096]{1,0:T(8,128)(2,1)}, u32[]{:S(2)}) copy-start(bf16[32,4096]{1,0:T(8,128)(2,1)} %param.13) | copy-start | bytes 786436
  7.9 17.6 %all-to-all-start = ((s32[32,1,8]{2,1,0:T(1,128)}), s32[32,1,8]{2,1,0:T(1,128)S(1)}, u32[]{:S(2)}, u32[]{:S(2)}) async-start(s32[32,1,8]{2,1,0:T(1,128)} %broadcast_in_dim.43), calls=%async_computation | async-start | bytes 32768 | tf_op jit(solution)/shard_map/all_to_all | solution.py:14
  26.4 9.2 all-to-all-start.1
  38.4 8.4 all-to-all-start.2
  46.9 13.8 %all-to-all-start.3 = ((bf16[4,16,4096]{2,1,0:T(8,128)(2,1)}), bf16[4,16,4096]{2,1,0:T(8,128)(2,1)S(1)}, u32[]{:S(2)}, u32[]{:S(2)}) async-start(bf16[4,16,4096]{2,1,0:T(8,128)(2,1)} %bitcast.11), calls=%async_computation.3 | async-start | bytes 1048576 | tf_op jit(solution)/shard_map/all_to_all | solution.py:133
  50.3 91.9 %reduce-scatter.4.cloned.1.call-start = ((), (), s32[]{:S(2)}) async-start(), calls=%async_computation.10 | async-start | bytes 10485760 | tf_op jit(solution)/shard_map/reduce_scatter | solution.py:52
  66.2 169.9 %copy-start.3 = (f32[4,4096]{1,0:T(4,128)S(1)}, f32[4,4096]{1,0:T(4,128)}, u32[]{:S(2)}) copy-start(f32[4,4096]{1,0:T(4,128)} %param.16) | copy-start | bytes 196612
  66.2 254.7 %copy-start.2 = (bf16[8,4096]{1,0:T(8,128)(2,1)S(1)}, bf16[8,4096]{1,0:T(8,128)(2,1)}, u32[]{:S(2)}) copy-start(bf16[8,4096]{1,0:T(8,128)(2,1)} %param.15) | copy-start | bytes 196612
  66.2 107.8 %reduce-scatter.6.cloned.1.call-start = ((), (), s32[]{:S(2)}) async-start(), calls=%async_computation.11 | async-start | bytes 2621440 | tf_op jit(solution)/shard_map/reduce_scatter | solution.py:52
  142.3 51.0 %reduce-scatter.8.cloned.1.call-start = ((), (), s32[]{:S(2)}) async-start(), calls=%async_computation.12 | async-start | bytes 786432 | tf_op jit(solution)/shard_map/reduce_scatter | solution.py:52
  174.0 62.0 %all-gather.5.cloned.1.call-start = ((), (), s32[]{:S(2)}) async-start(), calls=%async_computation.13 | async-start | bytes 2621440 | tf_op jit(solution)/shard_map/all_gather | solution.py:59
  203.5 117.4 %all-gather.7.cloned.1.call-start = ((), (), s32[]{:S(2)}) async-start(), calls=%async_computation.14 | async-start | bytes 10485760 | tf_op jit(solution)/shard_map/all_gather | solution.py:59
  362.7 130.7 %all-to-all-start.4 = ((bf16[32,1024,128]{2,1,0:T(8,128)(2,1)}), bf16[32,1024,128]{2,1,0:T(8,128)(2,1)}, u32[]{:S(2)}, u32[]{:S(2)}) async-start(bf16[32,1024,128]{2,1,0:T(8,128)(2,1)} %stack.6), calls=%async_computation.7 | async-start | bytes 16777216 | tf_op jit(solution)/shard_map/all_to_all | solution.py:162
  559.7 128.2 %all-to-all-start.5 = ((bf16[32,1024,128]{2,1,0:T(8,128)(2,1)}), bf16[32,1024,128]{2,1,0:T(8,128)(2,1)}, u32[]{:S(2)}, u32[]{:S(2)}) async-start(bf16[32,1024,128]{2,1,0:T(8,128)(2,1)} %stack.7), calls=%async_computation.8 | async-start | bytes 16777216 | tf_op jit(solution)/shard_map/all_to_all | solution.py:162
  911.8 14.7 %copy-start.1 = (bf16[32,4096]{1,0:T(8,128)(2,1)S(1)}, bf16[32,4096]{1,0:T(8,128)(2,1)}, u32[]{:S(2)}) copy-start(bf16[32,4096]{1,0:T(8,128)(2,1)} %param.13) | copy-start | bytes 786436
Sparse Core Ops, SparseCore 0:
  66.3 75.9 reduce-scatter.3
  144.7 29.2 reduce-scatter.5
  176.4 16.8 reduce-scatter.7
  203.6 32.3 all-gather.4
  237.6 83.2 all-gather.6
